TPU v7x, 32 devices: a whole 2x2x4 slice. The times are simulated.
32 devices in a mesh: rows: 16 (over z, y, x), cols: 2 (over core).
Axes of the slice: x: 2, y: 2, z: 4, core: 2. Of those that a mesh axis runs over, the one named last changes fastest.
Arguments:
- panel: float32 [2048, 32768], P('rows', 'cols'), may hold values from -0.03125 to 0.03125
- solved: float32 [32768, 64], P('cols'), may hold values from -6 to 6
- sketch: float32 [2048, 64], P('rows'), may hold values from -6 to 6
- inverses: float32 [2, 1024, 1024], P(None, 'rows', 'cols'), may hold values from -2 to 2, as said below
- coupling: float32 [1024, 1024], P('rows', 'cols'), may hold values from -0.1875 to 0.1875
- design: bfloat16 [32768, 2048], P('rows', 'cols'), may hold values from -0.125 to 0.125
- prior: float32 [32768, 64], P(('rows', 'cols')), may hold values from -6 to 6
Outputs:
- block_solution: float32 [2048, 64], P('rows')
- leverage: float32 [32768], P(('rows', 'cols'))
Inputs may be any that keep to these rules, and one draw needn't show every extreme that they name: `inverses`: each of the two blocks is upper triangular with a positive diagonal.
All inputs are finite; a program needn't handle non-finite values.
Results may differ from a plain program's by a relative error of at most 0.00063.
Values sent between devices are 32-bit elements; how exact they have to be, the bound alone decides.
A program may use at most 64 MiB of HBM per device.

v0:
```python
import jax
import jax.numpy as jnp
from jax import lax
from jax.sharding import PartitionSpec as P


def assemble(term):
    rows_here = lax.psum(term, "cols")
    return lax.all_gather(rows_here, "rows", axis=0, tiled=True)


def local(panel, solved, sketch, inverses, coupling, design, prior):
    highest = lax.Precision.HIGHEST
    partial_value = jnp.dot(panel, solved, precision=highest)
    local_right = sketch - lax.psum(partial_value, "cols")
    right = lax.all_gather(local_right, "rows", axis=0, tiled=True)
    blocks = right.shape[0] // 2
    width = inverses.shape[2]
    column = lax.axis_index("cols")
    offset = column * width

    def piece(vector):
        return lax.dynamic_slice_in_dim(vector, offset, width, 0)

    right_first = right[:blocks]
    right_last = right[blocks:]
    sketch_cols = right.shape[1]
    inverse_full = lax.all_gather(inverses[0], "cols", axis=1, tiled=True)
    coupling_full = lax.all_gather(coupling, "rows", axis=0, tiled=True)
    mixed = jnp.dot(inverse_full, coupling_full, precision=highest)
    term_last = jnp.dot(inverses[1], piece(right_last), precision=highest)
    term_first = jnp.dot(inverses[0], piece(right_first), precision=highest)
    joined = assemble(jnp.concatenate([term_last, term_first], axis=1))
    y_last = joined[:, :sketch_cols]
    partial_first = joined[:, sketch_cols:]
    correction = assemble(jnp.dot(mixed, piece(y_last), precision=highest))
    y_first = partial_first - correction
    solution = jnp.concatenate([y_first, y_last], axis=0)
    own_rows = sketch.shape[0]
    block_solution = lax.dynamic_slice_in_dim(
        solution, lax.axis_index("rows") * own_rows, own_rows, 0
    )
    design_cols = design.shape[1]
    rounded = lax.dynamic_slice_in_dim(solution, column * design_cols, design_cols, 0).astype(
        jnp.bfloat16
    )
    mine = lax.psum_scatter(
        jnp.dot(design, rounded, preferred_element_type=jnp.float32),
        "cols",
        scatter_dimension=0,
        tiled=True,
    )
    product = prior + mine
    leverage = jnp.mean(product * product, axis=1)
    return (block_solution, leverage)


def solution(mesh):
    in_specs = (
        P("rows", "cols"),
        P("cols", None),
        P("rows", None),
        P(None, "rows", "cols"),
        P("rows", "cols"),
        P("rows", "cols"),
        P(("rows", "cols"), None),
    )
    out_specs = (P("rows", None), P(("rows", "cols")))
    return jax.shard_map(local, mesh=mesh, in_specs=in_specs, out_specs=out_specs, check_vma=False)
```

profile of v0, /device:TPU:0, one launch (start us, length us, event | category | flops | bytes accessed | tf_op | source)
XLA Modules:
  0.0 179.0 jit_solution(4437025293409129676)
XLA Ops:
  7.2 0.0 all-gather.3.cloned.1.call-start
  7.2 0.7 all-gather.3.cloned.1.call-update
  7.9 0.0 reduce-scatter.2.cloned.1.call-start
  8.0 0.0 copy-start.2
  8.0 0.0 copy-start
  8.0 0.0 slice-start
  8.0 11.7 %fusion.20 = f32[128,64]{0,1:T(8,128)S(1)} fusion(f32[128,16384]{1,0:T(8,128)} %param.7, f32[16384,64]{0,1:T(8,128)} %param.8), kind=kOutput, calls=%fused_computation.30 | convolution fusion | flops 1610612736 | bytes 12615680 | tf_op jit(solution)/shard_map/dot_general | solution.py:14
  19.7 3.7 %psum.21 = f32[128,64]{0,1:T(8,128)S(1)} all-reduce(f32[128,64]{0,1:T(8,128)S(1)} %fusion.20), channel_id=1, replica_groups=mesh['rows'=16,'cols'=2] {'cols'}, use_global_device_ids=true, to_apply=%region_0.0 | all-reduce | flops 8192 | bytes 65536 | tf_op jit(solution)/shard_map/psum | solution.py:15
  23.5 0.0 copy-done.2
  23.5 46.7 %all_gather.15 = f32[2048,64]{0,1:T(8,128)S(1)} all-gather(f32[128,64]{0,1:T(8,128)S(1)} %sub.6), channel_id=1, replica_groups=mesh['rows'=16,'cols'=2] {'rows'}, dimensions={0}, use_global_device_ids=true | all-gather | bytes 557056 | tf_op jit(solution)/shard_map/all_gather | solution.py:16
  70.3 0.0 copy-done
  70.3 0.3 convolution_bitcast_fusion.1
  70.6 0.3 convolution_bitcast_fusion.2
  70.8 0.1 pad_maximum_fusion
  70.9 3.4 %psum.22 = f32[64,128]{1,0:T(8,128)S(1)} all-reduce(f32[64,128]{1,0:T(8,128)S(1)} %pad_maximum_fusion), channel_id=1, replica_groups=mesh['rows'=16,'cols'=2] {'cols'}, use_global_device_ids=true, to_apply=%region_1.0 | all-reduce | flops 8192 | bytes 65536 | tf_op jit(solution)/shard_map/psum | solution.py:8
  74.3 0.0 slice-done
  74.3 2.0 %all-gather = f32[1,64,1024]{2,1,0:T(8,128)S(1)} all-gather(f32[1,64,512]{2,1,0:T(8,128)S(1)} %slice-done), channel_id=2, replica_groups=mesh['rows'=16,'cols'=2] {'cols'}, dimensions={2}, use_global_device_ids=true | all-gather | bytes 393216 | tf_op jit(solution)/shard_map/all_gather | solution.py:28
  76.3 38.2 %all_gather.16 = f32[1024,128]{1,0:T(8,128)S(1)} all-gather(f32[64,128]{1,0:T(8,128)S(1)} %psum.22), channel_id=1, replica_groups=mesh['rows'=16,'cols'=2] {'rows'}, dimensions={0}, use_global_device_ids=true | all-gather | bytes 557056 | tf_op jit(solution)/shard_map/all_gather | solution.py:9
  114.6 0.0 all-gather.3.cloned.1.call-done
  114.6 3.0 %fusion.3 = f32[64,512]{1,0:T(8,128)S(1)} fusion(f32[1024,512]{1,0:T(8,128)} %all-gather.3.cloned.1.call-done, f32[1,64,1024]{2,1,0:T(8,128)S(1)} %all-gather), kind=kOutput, calls=%fused_computation.10 | convolution fusion | flops 402653184 | bytes 2490368 | tf_op jit(solution)/shard_map/dot_general | solution.py:30
  117.5 0.3 fusion.5
  117.8 3.4 %psum.23 = f32[64,64]{1,0:T(8,128)S(1)} all-reduce(f32[64,64]{1,0:T(8,128)S(1)} %fusion.5), channel_id=1, replica_groups=mesh['rows'=16,'cols'=2] {'cols'}, use_global_device_ids=true, to_apply=%region_2.0 | all-reduce | flops 4096 | bytes 32768 | tf_op jit(solution)/shard_map/psum | solution.py:8
  121.2 40.6 %all_gather.19 = f32[1024,64]{1,0:T(8,128)S(1)} all-gather(f32[64,64]{1,0:T(8,128)S(1)} %psum.23), channel_id=1, replica_groups=mesh['rows'=16,'cols'=2] {'rows'}, dimensions={0}, use_global_device_ids=true | all-gather | bytes 278528 | tf_op jit(solution)/shard_map/all_gather | solution.py:9
  161.9 0.0 copy-start.1
  161.9 0.2 slice_subtract_fusion
  162.1 4.5 %convolution_bitcast_fusion = f32[2048,64]{0,1:T(8,128)} fusion(bf16[2048,1024]{1,0:T(8,128)(2,1)} %param.12, s32[]{:T(128)S(6)} %select_n.13, f32[1024,64]{1,0:T(8,128)S(1)} %slice_subtract_fusion, f32[1024,64]{1,0:T(8,128)S(1)} %bitcast.22), kind=kOutput, calls=%fused_computation | convolution fusion | flops 268697600 | bytes 5242884 | tf_op jit(solution)/shard_map/dot_general | solution.py:48
  166.5 0.0 reduce-scatter.2.cloned.1.call-update
  166.6 0.7 copy.9
  167.3 3.2 %reduce-scatter.2.cloned.1.call-done = f32[1024,64]{0,1:T(8,128)} async-done(((f32[2048,64]{0,1:T(8,128)}), f32[1024,64]{0,1:T(8,128)}) %reduce-scatter.2.cloned.1.call-update) | async-done | bytes 262160 | tf_op jit(solution)/shard_map/reduce_scatter | solution.py:47
  170.5 0.0 copy-done.1
  170.5 1.0 multiply_reduce_fusion
  171.5 0.6 broadcast_multiply_fusion
  (3 shorter events, 0.1 us)
Async XLA Ops:
  7.2 107.4 %all-gather.3.cloned.1.call-start = ((), (), s32[]{:S(2)}) async-start(), calls=%async_computation.1 | async-start | bytes 2228224 | tf_op jit(solution)/shard_map/all_gather | solution.py:29
  7.9 162.6 %reduce-scatter.2.cloned.1.call-start = ((), (), s32[]{:S(2)}) async-start(), calls=%async_computation.2 | async-start | bytes 786432 | tf_op jit(solution)/shard_map/reduce_scatter | solution.py:47
  8.0 15.5 %copy-start.2 = (f32[128,64]{0,1:T(8,128)S(1)}, f32[128,64]{0,1:T(8,128)}, u32[]{:S(2)}) copy-start(f32[128,64]{0,1:T(8,128)} %param.9) | copy-start | bytes 98308
  8.0 62.3 %copy-start = (f32[2,64,512]{2,1,0:T(8,128)S(1)}, f32[2,64,512]{2,1,0:T(8,128)}, u32[]{:S(2)}) copy-start(f32[2,64,512]{2,1,0:T(8,128)} %param.10) | copy-start | bytes 786436
  8.0 66.3 %slice-start = ((f32[2,64,512]{2,1,0:T(8,128)}), f32[1,64,512]{2,1,0:T(8,128)S(1)}, s32[]{:S(2)}) async-start(f32[2,64,512]{2,1,0:T(8,128)} %param.10), calls=%async_computation.3 | async-start | bytes 262144 | tf_op jit(solution)/shard_map/slice | solution.py:32
  161.9 8.7 %copy-start.1 = (f32[1024,64]{0,1:T(8,128)S(1)}, f32[1024,64]{0,1:T(8,128)}, u32[]{:S(2)}) copy-start(f32[1024,64]{0,1:T(8,128)} %param.13) | copy-start | bytes 786436
Sparse Core Ops, SparseCore 0:
  10.7 65.2 all-gather.2
  166.7 3.7 reduce-scatter.1
where the time goes:
time: 179 us
  blocking collectives  138 us (77%)
  matrix products  20 us (11%)
  between operations  14.2 us (8%)
  waiting for transfers between devices  3.9 us (2%)
  other arithmetic  1.93 us (1%)
    all_gather x2, blocking collectives, assemble(): return lax.all_gather(rows_here, 'rows', axis=0, tiled=True)  78.9 us
    all_gather x1, blocking collectives, local(): right = lax.all_gather(local_right, 'rows', axis=0, tiled=True)  46.7 us
    dot_general x1, matrix products, local(): partial_value = jnp.dot(panel, solved, precision=highest)  11.7 us
    psum x2, blocking collectives, assemble(): rows_here = lax.psum(term, 'cols')  6.8 us
    dot_general x1, matrix products, local(): jnp.dot(design, rounded, preferred_element_type=jnp.float32)  4.48 us
    psum x1, blocking collectives, local(): local_right = sketch - lax.psum(partial_value, 'cols')  3.73 us
  transfers between devices with their start and end apart: 2, of which 1 were waited for; matrix products, arithmetic and copies ran while one was open for 7% of the time, Pallas kernels for 0%

commit v1 on v0

--- a/solution.py
+++ b/solution.py
@@ -1,7 +1,402 @@
+import functools
+
 import jax
 import jax.numpy as jnp
 from jax import lax
+from jax.experimental import pallas as pl
+from jax.experimental.pallas import tpu as pltpu
 from jax.sharding import PartitionSpec as P
+
+CHUNKS = 8
+NT = (((1,), (1,)), ((), ()))
+
+
+def nt(a, b, precision=None):
+    return lax.dot_general(a, b, NT, precision=precision, preferred_element_type=jnp.float32)
+
+
+def split(x):
+    high = x.astype(jnp.bfloat16)
+    low = (x - high.astype(jnp.float32)).astype(jnp.bfloat16)
+    return jnp.concatenate([high, low], axis=0)
+
+
+def kernel(
+    n,
+    panel, solved, sketch, inverses, coupling, design, prior,
+    out_solution, out_leverage,
+    panel_v, solved_v, sketch_v, inverses_v, coupling_v, design_v, prior_v,
+    acc, part_tx, part_rx, right_tx, right_last, right_first,
+    pair_tx, pair_rx, block_tx, gathered, stacked, y_half, sol_tx, sol_rx, prod_tx, prod_rx,
+    load_sem, pair_send, pair_recv, send_sem, recv_sem, first_recv, aux_send, aux_recv,
+):
+    r = lax.axis_index("rows")
+    c = lax.axis_index("cols")
+    peer = 1 - c
+    depth = panel.shape[1]
+    step = depth // CHUNKS
+    k, pr = sketch.shape
+    kh, kq = k // 2, k // 4
+    half = n // 2
+    quarter = n // 4
+    ir = pr // 2
+
+    def chunk(i):
+        at = pl.ds(pl.multiple_of(i * step, step), step)
+        return (
+            pltpu.make_async_copy(panel.at[:, at], panel_v.at[:, at], load_sem.at[0, i]),
+            pltpu.make_async_copy(solved.at[:, at], solved_v.at[:, at], load_sem.at[1, i]),
+        )
+
+    for i in range(CHUNKS):
+        for copy in chunk(i):
+            copy.start()
+    late = [
+        pltpu.make_async_copy(src, dst, load_sem.at[2, i])
+        for i, (src, dst) in enumerate(
+            (
+                (sketch, sketch_v),
+                (inverses, inverses_v),
+                (coupling, coupling_v),
+                (prior, prior_v),
+                (design, design_v),
+            )
+        )
+    ]
+    for copy in late:
+        copy.start()
+
+    barrier = pltpu.get_barrier_semaphore()
+
+    def greet(i, carry):
+        pl.semaphore_signal(
+            barrier, inc=1, device_id=((r + 1 + i // 2) % n, i % 2), device_id_type=pl.DeviceIdType.MESH
+        )
+        return carry
+
+    lax.fori_loop(0, 2 * n - 2, greet, 0)
+    pl.semaphore_signal(barrier, inc=1, device_id=(r, peer), device_id_type=pl.DeviceIdType.MESH)
+
+    acc[...] = jnp.zeros_like(acc)
+
+    def body(i, carry):
+        for copy in chunk(i):
+            copy.wait()
+        at = pl.ds(pl.multiple_of(i * step, step), step)
+        acc[...] += nt(split(solved_v[:, at]), split(panel_v[:, at]))
+        return carry
+
+    lax.fori_loop(0, CHUNKS, body, 0)
+    total = acc[...]
+    part = (total[:k, :pr] + total[k:, :pr]) + (total[:k, pr:] + total[k:, pr:])
+    pl.semaphore_wait(barrier, 2 * n - 1)
+
+    def to_peer(src, dst, which):
+        return pltpu.make_async_remote_copy(
+            src_ref=src,
+            dst_ref=dst,
+            send_sem=pair_send.at[which],
+            recv_sem=pair_recv.at[which],
+            device_id=(r, peer),
+            device_id_type=pl.DeviceIdType.MESH,
+        )
+
+    part_tx[...] = part
+    pairs = [to_peer(part_tx.at[pl.ds(pl.multiple_of(kh * peer, kh), kh)], part_rx, 0)]
+    pairs[0].start()
+    late[0].wait()
+    mine = pl.ds(pl.multiple_of(kh * c, kh), kh)
+    own = sketch_v[mine, :] - part_tx[mine, :]
+    pairs[0].wait_recv()
+    right_tx[...] = own - part_rx[...]
+
+    def spread(which, src, dst, core, i, recv):
+        to = (r + half + i) % n
+        here = jnp.logical_and(to == r, core == c)
+
+        @pl.when(here)
+        def _():
+            pltpu.make_async_copy(src, dst, recv).start()
+
+        @pl.when(jnp.logical_not(here))
+        def _():
+            pltpu.make_async_remote_copy(
+                src_ref=src,
+                dst_ref=dst,
+                send_sem=send_sem.at[which, i],
+                recv_sem=recv,
+                device_id=(to, core),
+                device_id_type=pl.DeviceIdType.MESH,
+            ).start()
+
+    def settle(which, src, dst, core, i, recv):
+        to = (r + half + i) % n
+        here = jnp.logical_and(to == r, core == c)
+
+        @pl.when(jnp.logical_not(here))
+        def _():
+            pltpu.make_async_remote_copy(
+                src_ref=src,
+                dst_ref=dst,
+                send_sem=send_sem.at[which, i],
+                recv_sem=recv,
+                device_id=(to, core),
+                device_id_type=pl.DeviceIdType.MESH,
+            ).wait_send()
+
+    def everywhere(act, which, src, dst, core, recv):
+        def one(i, carry):
+            act(which, src, dst, core, i, recv)
+            return carry
+
+        lax.fori_loop(0, n, one, 0)
+
+    last_at = pl.ds(pl.multiple_of(pr * (r % quarter), pr), pr)
+    last_args = (0, right_tx, right_last.at[mine, last_at], (r % half) // quarter, recv_sem.at[0])
+
+    def first_rows(act_local, act_remote):
+        for i in range(4):
+            to, core = (2 * r + i // 2) % n, i % 2
+            here = jnp.logical_and(to == r, core == c)
+
+            @pl.when(here)
+            def _():
+                act_local(pltpu.make_async_copy(right_tx, right_first.at[c], first_recv))
+
+            @pl.when(jnp.logical_not(here))
+            def _():
+                act_remote(
+                    pltpu.make_async_remote_copy(
+                        src_ref=right_tx,
+                        dst_ref=right_first.at[c],
+                        send_sem=send_sem.at[0, i],
+                        recv_sem=first_recv,
+                        device_id=(to, core),
+                        device_id_type=pl.DeviceIdType.MESH,
+                    )
+                )
+
+    @pl.when(r >= half)
+    def _():
+        everywhere(spread, *last_args)
+
+    @pl.when(r < half)
+    def _():
+        first_rows(lambda copy: copy.start(), lambda copy: copy.start())
+
+    def arrived(ref, sem):
+        pltpu.make_async_copy(ref, ref, sem).wait()
+
+    lane = lax.broadcasted_iota(jnp.int32, (kh, pr), 1)
+    lane_q = lax.broadcasted_iota(jnp.int32, (kq, pr), 1)
+    part_at = pl.ds(pl.multiple_of(kq * c, kq), kq)
+    peer_at = pl.ds(pl.multiple_of(kq * peer, kq), kq)
+
+    def unfold(a, b):
+        low = jnp.where(lane < ir, a, pltpu.roll(b, ir, 1))
+        high = jnp.where(lane < ir, pltpu.roll(a, ir, 1), b)
+        return jnp.concatenate([low, high], axis=0)
+
+    def pair_sum(operand, weights, which):
+        doubled = jnp.concatenate([weights, weights], axis=0)
+        whole = nt(operand, doubled, lax.Precision.HIGHEST)
+        pair_tx[which] = jnp.where(lane < ir, whole[:kh], whole[kh:])
+        copy = to_peer(pair_tx.at[which, peer_at], pair_rx.at[which], which + 1)
+        copy.start()
+        pairs.append(copy)
+        copy.wait_recv()
+        return pair_tx[which, part_at, :] + pair_rx[which]
+
+    def load_stacked(which):
+        for s in range(quarter):
+            a = gathered[which, half * c + 2 * s]
+            b = gathered[which, half * c + 2 * s + 1]
+            stacked[:, s * pr : (s + 1) * pr] = unfold(a, b)
+        return stacked[...]
+
+    def block_args(which, core):
+        return (
+            which + 1,
+            block_tx.at[which],
+            gathered.at[which, r, part_at],
+            core,
+            recv_sem.at[which + 1],
+        )
+
+    side = r // half
+    half_at = pl.ds(pl.multiple_of(half * c, half), half)
+
+    late[1].wait()
+    arrived(right_last, recv_sem.at[0])
+    block_tx[0] = pair_sum(right_last[...], inverses_v[1], 0)
+    everywhere(spread, *block_args(0, side))
+    late[2].wait()
+    arrived(gathered.at[0, half_at], recv_sem.at[1])
+
+    def handover():
+        return pltpu.make_async_remote_copy(
+            src_ref=gathered.at[0, pl.ds(0, half)],
+            dst_ref=gathered.at[0, pl.ds(0, half)],
+            send_sem=aux_send.at[0],
+            recv_sem=aux_recv.at[0],
+            device_id=(r, peer),
+            device_id_type=pl.DeviceIdType.MESH,
+        )
+
+    @pl.when(c == 0)
+    def _():
+        handover().start()
+
+    bent = pair_sum(load_stacked(0), coupling_v[...], 1)
+    arrived(right_first, first_recv)
+    a, b = right_first[0, part_at, :], right_first[1, part_at, :]
+    even = jnp.where(lane_q < ir, a, pltpu.roll(b, ir, 1))
+    odd = jnp.where(lane_q < ir, pltpu.roll(a, ir, 1), b)
+    block_tx[1] = jnp.where(r % 2 == 0, even, odd) - bent
+    everywhere(spread, *block_args(1, side))
+    arrived(gathered.at[1, half_at], recv_sem.at[2])
+
+    block_tx[2] = pair_sum(load_stacked(1), inverses_v[0], 2)
+    everywhere(spread, *block_args(2, 0))
+    late[3].wait()
+    late[4].wait()
+
+    sol_copy = pltpu.make_async_remote_copy(
+        src_ref=sol_tx,
+        dst_ref=sol_rx,
+        send_sem=aux_send.at[1],
+        recv_sem=aux_recv.at[1],
+        device_id=(r, peer),
+        device_id_type=pl.DeviceIdType.MESH,
+    )
+
+    def finish(which):
+        for s in range(half):
+            both = unfold(gathered[which, 2 * s], gathered[which, 2 * s + 1])
+            y_half[:, s * pr : (s + 1) * pr] = both.astype(jnp.bfloat16)
+        at = 2 * (r % half)
+
+        @pl.when(side == c)
+        def _():
+            both = unfold(gathered[which, at], gathered[which, at + 1])
+            sol_tx[...] = both
+            sol_copy.start()
+            out_solution[...] = both
+
+    @pl.when(c == 0)
+    def _():
+        arrived(gathered.at[2], recv_sem.at[3])
+        finish(2)
+
+    @pl.when(c == 1)
+    def _():
+        handover().wait_recv()
+        finish(0)
+
+    rows_here = prior.shape[1]
+
+    def product(which):
+        at = pl.ds(pl.multiple_of(rows_here * which, rows_here), rows_here)
+        return nt(y_half[...], design_v[at, :])
+
+    prod_copy = pltpu.make_async_remote_copy(
+        src_ref=prod_tx,
+        dst_ref=prod_rx,
+        send_sem=aux_send.at[2],
+        recv_sem=aux_recv.at[2],
+        device_id=(r, peer),
+        device_id_type=pl.DeviceIdType.MESH,
+    )
+    prod_tx[...] = product(peer)
+    prod_copy.start()
+    held = product(c) + prior_v[...]
+    prod_copy.wait_recv()
+    whole = held + prod_rx[...]
+    out_leverage[...] = jnp.mean(whole * whole, axis=0, keepdims=True)
+
+    @pl.when(side != c)
+    def _():
+        sol_copy.wait_recv()
+        out_solution[...] = sol_rx[...]
+
+    @pl.when(side == c)
+    def _():
+        sol_copy.wait_send()
+
+    prod_copy.wait_send()
+
+    @pl.when(c == 0)
+    def _():
+        handover().wait_send()
+
+    for copy in pairs:
+        copy.wait_send()
+
+    @pl.when(r >= half)
+    def _():
+        everywhere(settle, *last_args)
+
+    @pl.when(r < half)
+    def _():
+        first_rows(lambda copy: None, lambda copy: copy.wait_send())
+
+    for which, core in ((0, side), (1, side), (2, 0)):
+        everywhere(settle, *block_args(which, core))
+
+
+def fused(n, panel, solved, sketch, inverses, coupling, design, prior):
+    k = sketch.shape[1]
+    pr, depth = panel.shape
+    rows_here = prior.shape[0]
+    width = inverses.shape[2]
+    kh, kq = k // 2, k // 4
+    f32 = jnp.float32
+    out_solution, out_leverage = pl.pallas_call(
+        functools.partial(kernel, n),
+        out_shape=(
+            jax.ShapeDtypeStruct((k, pr), f32),
+            jax.ShapeDtypeStruct((1, rows_here), f32),
+        ),
+        in_specs=[pl.BlockSpec(memory_space=pl.ANY)] * 7,
+        out_specs=[pl.BlockSpec(memory_space=pltpu.VMEM)] * 2,
+        scratch_shapes=[
+            pltpu.VMEM((pr, depth), f32),
+            pltpu.VMEM((k, depth), f32),
+            pltpu.VMEM((k, pr), f32),
+            pltpu.VMEM(inverses.shape, f32),
+            pltpu.VMEM(coupling.shape, f32),
+            pltpu.VMEM(design.shape, design.dtype),
+            pltpu.VMEM((k, rows_here), f32),
+            pltpu.VMEM((2 * k, 2 * pr), f32),
+            pltpu.VMEM((k, pr), f32),
+            pltpu.VMEM((kh, pr), f32),
+            pltpu.VMEM((kh, pr), f32),
+            pltpu.VMEM((k, width), f32),
+            pltpu.VMEM((2, kh, pr), f32),
+            pltpu.VMEM((3, kh, pr), f32),
+            pltpu.VMEM((3, kq, pr), f32),
+            pltpu.VMEM((3, kq, pr), f32),
+            pltpu.VMEM((3, n, kh, pr), f32),
+            pltpu.VMEM((k, width), f32),
+            pltpu.VMEM((k, 2 * width), jnp.bfloat16),
+            pltpu.VMEM((k, pr), f32),
+            pltpu.VMEM((k, pr), f32),
+            pltpu.VMEM((k, rows_here), f32),
+            pltpu.VMEM((k, rows_here), f32),
+            pltpu.SemaphoreType.DMA((3, CHUNKS)),
+            pltpu.SemaphoreType.DMA((4,)),
+            pltpu.SemaphoreType.DMA((4,)),
+            pltpu.SemaphoreType.DMA((4, n)),
+            pltpu.SemaphoreType.DMA((4,)),
+            pltpu.SemaphoreType.DMA,
+            pltpu.SemaphoreType.DMA((3,)),
+            pltpu.SemaphoreType.DMA((3,)),
+        ],
+        compiler_params=pltpu.CompilerParams(
+            collective_id=0, has_side_effects=True, vmem_limit_bytes=48 * 1024 * 1024
+        ),
+    )(panel, solved.T, sketch.T, inverses, coupling, design, prior.T)
+    return out_solution.T, out_leverage.reshape(rows_here)
 
 
 def assemble(term):
@@ -55,6 +450,13 @@
     return (block_solution, leverage)
 
 
+def local_or_fused(rows, panel, solved, sketch, inverses, coupling, design, prior):
+    args = (panel, solved, sketch, inverses, coupling, design, prior)
+    pr, depth = panel.shape
+    fits = pr == 128 and depth % (CHUNKS * 128) == 0 and sketch.shape[1] % 32 == 0
+    return fused(rows, *args) if fits else local(*args)
+
+
 def solution(mesh):
     in_specs = (
         P("rows", "cols"),
@@ -66,4 +468,8 @@
         P(("rows", "cols"), None),
     )
     out_specs = (P("rows", None), P(("rows", "cols")))
-    return jax.shard_map(local, mesh=mesh, in_specs=in_specs, out_specs=out_specs, check_vma=False)
+    rows, cols = mesh.shape["rows"], mesh.shape["cols"]
+    step = local
+    if cols == 2 and rows % 4 == 0:
+        step = functools.partial(local_or_fused, rows)
+    return jax.shard_map(step, mesh=mesh, in_specs=in_specs, out_specs=out_specs, check_vma=False)

time: 179 us -> 49.1 us (0.27)
  blocking collectives: 138 us -> 0 us
  Pallas kernels: 0 us -> 41.2 us
  matrix products: 20 us -> 0 us
  between operations: 14.2 us -> 0.65 us
  local copies, waits for them, and re-layouts: 0.76 us -> 6.95 us
  waiting for transfers between devices: 3.9 us -> 0 us
  other arithmetic: 1.93 us -> 0 us
    all_gather x4 -> x0, blocking collectives: 128 us -> none  [the longest x2 78.9 us: assemble(): return lax.all_gather(rows_here, 'rows', axis=0, tiled=True)]
    pallas_call x0 -> x1, Pallas kernels: none -> 41.2 us  [fused(): pl.pallas_call(functools.partial(kernel, n), out_shape=(jax.ShapeDtypeStr...]
    dot_general x6 -> x0, matrix products: 20 us -> none  [the longest x1 11.7 us: local(): partial_value = jnp.dot(panel, solved, precision=highest)]
    psum x3 -> x0, blocking collectives: 10.5 us -> none  [the longest x2 6.8 us: assemble(): rows_here = lax.psum(term, 'cols')]
    unnamed x7 -> x12, local copies, waits for them, and re-layouts: 0.71 us -> 6.95 us
    reduce_scatter x1 -> x0, waiting for transfers between devices: 3.2 us -> none  [local(): lax.psum_scatter(jnp.dot(design, rounded, preferred_element_type=jnp.floa...]
  transfers between devices with their start and end apart: 2 -> 0, of which waited for: 1 -> 0; matrix products, arithmetic and copies ran while one was open for 7% -> 0% of each run, Pallas kernels for 0% -> 0%
where the time goes in v1:
time: 49.1 us; the launch traced here: 48.8 us
  Pallas kernels  41.2 us (84%)
  local copies, waits for them, and re-layouts  6.95 us (14%)
  between operations  0.65 us (1%)
    pallas_call x1, Pallas kernels, fused(): pl.pallas_call(functools.partial(kernel, n), out_shape=(jax.ShapeDtypeStr...  41.2 us
    unnamed x12, local copies, waits for them, and re-layouts  6.95 us

profile of v1, /device:TPU:0, one launch (start us, length us, event | category | flops | bytes accessed | tf_op | source)
XLA Modules:
  0.0 48.8 jit_solution(4963930444949870501)
XLA Ops:
  0.6 0.0 copy-start
  0.6 2.2 %copy-done = f32[16384,64]{0,1:T(8,128)S(1)} copy-done((f32[16384,64]{0,1:T(8,128)S(1)}, f32[16384,64]{0,1:T(8,128)}, u32[]{:S(2)}) %copy-start) | copy-done | bytes 4194328
  2.8 0.0 copy-start.1
  2.8 0.9 %copy-done.1 = f32[2,64,512]{2,1,0:T(8,128)S(1)} copy-done((f32[2,64,512]{2,1,0:T(8,128)S(1)}, f32[2,64,512]{2,1,0:T(8,128)}, u32[]{:S(2)}) %copy-start.1) | copy-done | bytes 262168
  3.8 0.0 copy-start.2
  3.8 0.9 %copy-done.2 = f32[1024,64]{0,1:T(8,128)S(1)} copy-done((f32[1024,64]{0,1:T(8,128)S(1)}, f32[1024,64]{0,1:T(8,128)}, u32[]{:S(2)}) %copy-start.2) | copy-done | bytes 262168
  4.7 0.0 copy-start.3
  4.7 0.9 %copy-done.3 = f32[64,512]{1,0:T(8,128)S(1)} copy-done((f32[64,512]{1,0:T(8,128)S(1)}, f32[64,512]{1,0:T(8,128)}, u32[]{:S(2)}) %copy-start.3) | copy-done | bytes 131096
  5.6 0.0 copy-start.4
  5.6 0.8 %copy-done.4 = f32[128,64]{0,1:T(8,128)S(1)} copy-done((f32[128,64]{0,1:T(8,128)S(1)}, f32[128,64]{0,1:T(8,128)}, u32[]{:S(2)}) %copy-start.4) | copy-done | bytes 32792
  6.4 41.2 %shard_map.86 = (f32[64,128]{1,0:T(8,128)S(1)}, f32[1,1024]{1,0:T(1,128)S(1)}) custom-call(f32[128,16384]{1,0:T(8,128)} %panel.1, f32[64,16384]{1,0:T(8,128)S(1)} %bitcast.5, f32[64,128]{1,0:T(8,128)S(1)} %bitcast.7, f32[2,64,512]{2,1,0:T(8,128)S(1)} %copy-done.1, f32[64,512]{1,0:T(8,128)S(1)} %copy-done.3, bf16[2048,1024]{1,0:T(8,128)(2,1)} %design.1, ...), custom_call_target="tpu_custom_call" | custom-call | tf_op jit(solution)/shard_map/pallas_call | solution.py:354
  47.6 0.6 %copy.11 = f32[128,64]{0,1:T(8,128)} copy(f32[128,64]{0,1:T(8,128)S(1)} %bitcast.8) | data formatting | bytes 65536
  48.2 0.6 %copy.12 = f32[1024]{0:T(1024)} copy(f32[1024]{0:T(1024)S(1)} %bitcast.9) | data formatting | bytes 8192
Async XLA Ops:
  0.6 2.2 %copy-start = (f32[16384,64]{0,1:T(8,128)S(1)}, f32[16384,64]{0,1:T(8,128)}, u32[]{:S(2)}) copy-start(f32[16384,64]{0,1:T(8,128)} %param.8) | copy-start | bytes 12582916
  2.8 0.9 %copy-start.1 = (f32[2,64,512]{2,1,0:T(8,128)S(1)}, f32[2,64,512]{2,1,0:T(8,128)}, u32[]{:S(2)}) copy-start(f32[2,64,512]{2,1,0:T(8,128)} %inverses.1) | copy-start | bytes 786436
  3.8 0.9 %copy-start.2 = (f32[1024,64]{0,1:T(8,128)S(1)}, f32[1024,64]{0,1:T(8,128)}, u32[]{:S(2)}) copy-start(f32[1024,64]{0,1:T(8,128)} %param.13) | copy-start | bytes 786436
  4.7 0.9 %copy-start.3 = (f32[64,512]{1,0:T(8,128)S(1)}, f32[64,512]{1,0:T(8,128)}, u32[]{:S(2)}) copy-start(f32[64,512]{1,0:T(8,128)} %coupling.1) | copy-start | bytes 393220
  5.6 0.8 %copy-start.4 = (f32[128,64]{0,1:T(8,128)S(1)}, f32[128,64]{0,1:T(8,128)}, u32[]{:S(2)}) copy-start(f32[128,64]{0,1:T(8,128)} %param.9) | copy-start | bytes 98308

commit v2 on v1

--- a/solution.py
+++ b/solution.py
@@ -27,7 +27,7 @@
     out_solution, out_leverage,
     panel_v, solved_v, sketch_v, inverses_v, coupling_v, design_v, prior_v,
     acc, part_tx, part_rx, right_tx, right_last, right_first,
-    pair_tx, pair_rx, block_tx, gathered, stacked, y_half, sol_tx, sol_rx, prod_tx, prod_rx,
+    pair_tx, pair_rx, block_tx, gathered, stacked, y_half, sol_tx, sol_rx, prod_tx, prod_rx, split_v,
     load_sem, pair_send, pair_recv, send_sem, recv_sem, first_recv, aux_send, aux_recv,
 ):
     r = lax.axis_index("rows")
@@ -198,8 +198,9 @@
         return jnp.concatenate([low, high], axis=0)
 
     def pair_sum(operand, weights, which):
-        doubled = jnp.concatenate([weights, weights], axis=0)
-        whole = nt(operand, doubled, lax.Precision.HIGHEST)
+        terms = nt(split(operand), weights)
+        terms = terms[:k] + terms[k:]
+        whole = terms[:, :pr] + terms[:, pr:]
         pair_tx[which] = jnp.where(lane < ir, whole[:kh], whole[kh:])
         copy = to_peer(pair_tx.at[which, peer_at], pair_rx.at[which], which + 1)
         copy.start()
@@ -227,10 +228,13 @@
     half_at = pl.ds(pl.multiple_of(half * c, half), half)
 
     late[1].wait()
+    late[2].wait()
+    for i, weights in enumerate((inverses_v[1], coupling_v[...], inverses_v[0])):
+        split_v[i] = split(jnp.concatenate([weights, weights], axis=0))
+
     arrived(right_last, recv_sem.at[0])
-    block_tx[0] = pair_sum(right_last[...], inverses_v[1], 0)
+    block_tx[0] = pair_sum(right_last[...], split_v[0], 0)
     everywhere(spread, *block_args(0, side))
-    late[2].wait()
     arrived(gathered.at[0, half_at], recv_sem.at[1])
 
     def handover():
@@ -247,7 +251,7 @@
     def _():
         handover().start()
 
-    bent = pair_sum(load_stacked(0), coupling_v[...], 1)
+    bent = pair_sum(load_stacked(0), split_v[1], 1)
     arrived(right_first, first_recv)
     a, b = right_first[0, part_at, :], right_first[1, part_at, :]
     even = jnp.where(lane_q < ir, a, pltpu.roll(b, ir, 1))
@@ -256,7 +260,7 @@
     everywhere(spread, *block_args(1, side))
     arrived(gathered.at[1, half_at], recv_sem.at[2])
 
-    block_tx[2] = pair_sum(load_stacked(1), inverses_v[0], 2)
+    block_tx[2] = pair_sum(load_stacked(1), split_v[2], 2)
     everywhere(spread, *block_args(2, 0))
     late[3].wait()
     late[4].wait()
@@ -383,6 +387,7 @@
             pltpu.VMEM((k, pr), f32),
             pltpu.VMEM((k, rows_here), f32),
             pltpu.VMEM((k, rows_here), f32),
+            pltpu.VMEM((3, 2 * pr, width), jnp.bfloat16),
             pltpu.SemaphoreType.DMA((3, CHUNKS)),
             pltpu.SemaphoreType.DMA((4,)),
             pltpu.SemaphoreType.DMA((4,)),
@@ -393,7 +398,7 @@
             pltpu.SemaphoreType.DMA((3,)),
         ],
         compiler_params=pltpu.CompilerParams(
-            collective_id=0, has_side_effects=True, vmem_limit_bytes=48 * 1024 * 1024
+            collective_id=0, has_side_effects=True, vmem_limit_bytes=60 * 1024 * 1024
         ),
     )(panel, solved.T, sketch.T, inverses, coupling, design, prior.T)
     return out_solution.T, out_leverage.reshape(rows_here)

time: 49.1 us -> 44.4 us (0.904)
  local copies, waits for them, and re-layouts: 6.95 us -> 2.65 us
    unnamed x12 -> x2, local copies, waits for them, and re-layouts: 6.95 us -> 2.65 us
where the time goes in v2:
time: 44.4 us; the launch traced here: 44.2 us
  Pallas kernels  40.9 us (92%)
  local copies, waits for them, and re-layouts  2.65 us (6%)
  between operations  0.64 us (1%)
    pallas_call x1, Pallas kernels, fused(): pl.pallas_call(functools.partial(kernel, n), out_shape=(jax.ShapeDtypeStr...  40.9 us
    unnamed x2, local copies, waits for them, and re-layouts  2.65 us

profile of v2, /device:TPU:0, one launch (start us, length us, event | category | flops | bytes accessed | tf_op | source)
XLA Modules:
  0.0 44.2 jit_solution(10333137897793487931)
XLA Ops:
  0.6 40.9 %shard_map.86 = (f32[64,128]{1,0:T(8,128)}, f32[1,1024]{1,0:T(1,128)}) custom-call(f32[128,16384]{1,0:T(8,128)} %panel.1, f32[64,16384]{1,0:T(8,128)} %bitcast.5, f32[64,128]{1,0:T(8,128)} %bitcast.7, f32[2,64,512]{2,1,0:T(8,128)} %inverses.1, f32[64,512]{1,0:T(8,128)} %coupling.1, bf16[2048,1024]{1,0:T(8,128)(2,1)} %design.1, f32[64,1024]{1,0:T(8,128)} %bitcast.6), custom_call_target="tpu_custom_call" | custom-call | tf_op jit(solution)/shard_map/pallas_call | solution.py:358
  41.5 1.4 %copy.11 = f32[128,64]{0,1:T(8,128)} copy(f32[128,64]{0,1:T(8,128)} %bitcast.8) | data formatting | bytes 65536
  42.9 1.3 %copy.12 = f32[1024]{0:T(1024)} copy(f32[1024]{0:T(1024)} %bitcast.9) | data formatting | bytes 8192

commit v3 on v2

--- a/solution.py
+++ b/solution.py
@@ -29,6 +29,7 @@
     acc, part_tx, part_rx, right_tx, right_last, right_first,
     pair_tx, pair_rx, block_tx, gathered, stacked, y_half, sol_tx, sol_rx, prod_tx, prod_rx, split_v,
     load_sem, pair_send, pair_recv, send_sem, recv_sem, first_recv, aux_send, aux_recv,
+    cross_sem,
 ):
     r = lax.axis_index("rows")
     c = lax.axis_index("cols")
@@ -110,8 +111,40 @@
     pairs[0].wait_recv()
     right_tx[...] = own - part_rx[...]
 
+    side = r // half
+    other = (r + half) % n
+
+    def target(i):
+        return half * side + (r % half + i) % half
+
+    def across(which, src, dst, core):
+        return pltpu.make_async_remote_copy(
+            src_ref=src,
+            dst_ref=dst,
+            send_sem=send_sem.at[which, half],
+            recv_sem=cross_sem.at[which],
+            device_id=(other, core),
+            device_id_type=pl.DeviceIdType.MESH,
+        )
+
+    def relay(which, ref, act):
+        def one(i, carry):
+            act(
+                pltpu.make_async_remote_copy(
+                    src_ref=ref,
+                    dst_ref=ref,
+                    send_sem=send_sem.at[which, half + i],
+                    recv_sem=recv_sem.at[which],
+                    device_id=(target(i), c),
+                    device_id_type=pl.DeviceIdType.MESH,
+                )
+            )
+            return carry
+
+        lax.fori_loop(1, half, one, 0)
+
     def spread(which, src, dst, core, i, recv):
-        to = (r + half + i) % n
+        to = target(i)
         here = jnp.logical_and(to == r, core == c)
 
         @pl.when(here)
@@ -130,7 +163,7 @@
             ).start()
 
     def settle(which, src, dst, core, i, recv):
-        to = (r + half + i) % n
+        to = target(i)
         here = jnp.logical_and(to == r, core == c)
 
         @pl.when(jnp.logical_not(here))
@@ -149,7 +182,7 @@
             act(which, src, dst, core, i, recv)
             return carry
 
-        lax.fori_loop(0, n, one, 0)
+        lax.fori_loop(0, half, one, 0)
 
     last_at = pl.ds(pl.multiple_of(pr * (r % quarter), pr), pr)
     last_args = (0, right_tx, right_last.at[mine, last_at], (r % half) // quarter, recv_sem.at[0])
@@ -169,7 +202,7 @@
                     pltpu.make_async_remote_copy(
                         src_ref=right_tx,
                         dst_ref=right_first.at[c],
-                        send_sem=send_sem.at[0, i],
+                        send_sem=send_sem.at[4, i],
                         recv_sem=first_recv,
                         device_id=(to, core),
                         device_id_type=pl.DeviceIdType.MESH,
@@ -178,6 +211,7 @@
 
     @pl.when(r >= half)
     def _():
+        across(*last_args[:4]).start()
         everywhere(spread, *last_args)
 
     @pl.when(r < half)
@@ -186,6 +220,20 @@
 
     def arrived(ref, sem):
         pltpu.make_async_copy(ref, ref, sem).wait()
+
+    relays_last = jnp.logical_and(r < half, c == (r % half) // quarter)
+    last_ref = right_last.at[:, last_at]
+
+    def blocks_in(which):
+        @pl.when(c == side)
+        def _():
+            arrived(gathered.at[which, half_at], recv_sem.at[which + 1])
+
+        @pl.when(c != side)
+        def _():
+            arrived(gathered.at[which, other], cross_sem.at[which + 1])
+            relay(which + 1, gathered.at[which, other], lambda copy: copy.start())
+            arrived(gathered.at[which, pl.ds(0, half - 1)], recv_sem.at[which + 1])
 
     lane = lax.broadcasted_iota(jnp.int32, (kh, pr), 1)
     lane_q = lax.broadcasted_iota(jnp.int32, (kq, pr), 1)
@@ -224,7 +272,6 @@
             recv_sem.at[which + 1],
         )
 
-    side = r // half
     half_at = pl.ds(pl.multiple_of(half * c, half), half)
 
     late[1].wait()
@@ -232,10 +279,20 @@
     for i, weights in enumerate((inverses_v[1], coupling_v[...], inverses_v[0])):
         split_v[i] = split(jnp.concatenate([weights, weights], axis=0))
 
-    arrived(right_last, recv_sem.at[0])
+    @pl.when(relays_last)
+    def _():
+        arrived(last_ref, cross_sem.at[0])
+        relay(0, last_ref, lambda copy: copy.start())
+        arrived(right_last.at[:, pl.ds(0, right_last.shape[1] - pr)], recv_sem.at[0])
+
+    @pl.when(jnp.logical_not(relays_last))
+    def _():
+        arrived(right_last, recv_sem.at[0])
+
     block_tx[0] = pair_sum(right_last[...], split_v[0], 0)
+    across(*block_args(0, side)[:4]).start()
     everywhere(spread, *block_args(0, side))
-    arrived(gathered.at[0, half_at], recv_sem.at[1])
+    blocks_in(0)
 
     def handover():
         return pltpu.make_async_remote_copy(
@@ -257,10 +314,12 @@
     even = jnp.where(lane_q < ir, a, pltpu.roll(b, ir, 1))
     odd = jnp.where(lane_q < ir, pltpu.roll(a, ir, 1), b)
     block_tx[1] = jnp.where(r % 2 == 0, even, odd) - bent
+    across(*block_args(1, side)[:4]).start()
     everywhere(spread, *block_args(1, side))
-    arrived(gathered.at[1, half_at], recv_sem.at[2])
+    blocks_in(1)
 
     block_tx[2] = pair_sum(load_stacked(1), split_v[2], 2)
+    across(*block_args(2, 0)[:4]).start()
     everywhere(spread, *block_args(2, 0))
     late[3].wait()
     late[4].wait()
@@ -289,7 +348,9 @@
 
     @pl.when(c == 0)
     def _():
-        arrived(gathered.at[2], recv_sem.at[3])
+        arrived(gathered.at[2, other], cross_sem.at[3])
+        relay(3, gathered.at[2, other], lambda copy: copy.start())
+        arrived(gathered.at[2, pl.ds(0, n - 1)], recv_sem.at[3])
         finish(2)
 
     @pl.when(c == 1)
@@ -338,14 +399,29 @@
 
     @pl.when(r >= half)
     def _():
+        across(*last_args[:4]).wait_send()
         everywhere(settle, *last_args)
 
+    @pl.when(relays_last)
+    def _():
+        relay(0, last_ref, lambda copy: copy.wait_send())
+
     @pl.when(r < half)
     def _():
         first_rows(lambda copy: None, lambda copy: copy.wait_send())
 
     for which, core in ((0, side), (1, side), (2, 0)):
+        across(*block_args(which, core)[:4]).wait_send()
         everywhere(settle, *block_args(which, core))
+
+    @pl.when(c != side)
+    def _():
+        for which in (0, 1):
+            relay(which + 1, gathered.at[which, other], lambda copy: copy.wait_send())
+
+    @pl.when(c == 0)
+    def _():
+        relay(3, gathered.at[2, other], lambda copy: copy.wait_send())
 
 
 def fused(n, panel, solved, sketch, inverses, coupling, design, prior):
@@ -391,11 +467,12 @@
             pltpu.SemaphoreType.DMA((3, CHUNKS)),
             pltpu.SemaphoreType.DMA((4,)),
             pltpu.SemaphoreType.DMA((4,)),
-            pltpu.SemaphoreType.DMA((4, n)),
+            pltpu.SemaphoreType.DMA((5, n)),
             pltpu.SemaphoreType.DMA((4,)),
             pltpu.SemaphoreType.DMA,
             pltpu.SemaphoreType.DMA((3,)),
             pltpu.SemaphoreType.DMA((3,)),
+            pltpu.SemaphoreType.DMA((4,)),
         ],
         compiler_params=pltpu.CompilerParams(
             collective_id=0, has_side_effects=True, vmem_limit_bytes=60 * 1024 * 1024

time: 44.4 us -> 45.1 us (1.016)
  Pallas kernels: 40.9 us -> 41.6 us
    pallas_call x1, Pallas kernels: 40.9 us -> 41.6 us  [fused(): pl.pallas_call(functools.partial(kernel, n), out_shape=(jax.ShapeDtypeStr...]
where the time goes in v3:
time: 45.1 us; the launch traced here: 44.9 us
  Pallas kernels  41.6 us (92%)
  local copies, waits for them, and re-layouts  2.65 us (6%)
  between operations  0.64 us (1%)
    pallas_call x1, Pallas kernels, fused(): pl.pallas_call(functools.partial(kernel, n), out_shape=(jax.ShapeDtypeStr...  41.6 us
    unnamed x2, local copies, waits for them, and re-layouts  2.65 us

profile of v3, /device:TPU:0, one launch (start us, length us, event | category | flops | bytes accessed | tf_op | source)
XLA Modules:
  0.0 44.9 jit_solution(7680724596268270756)
XLA Ops:
  0.6 41.6 %shard_map.86 = (f32[64,128]{1,0:T(8,128)}, f32[1,1024]{1,0:T(1,128)}) custom-call(f32[128,16384]{1,0:T(8,128)} %panel.1, f32[64,16384]{1,0:T(8,128)} %bitcast.5, f32[64,128]{1,0:T(8,128)} %bitcast.7, f32[2,64,512]{2,1,0:T(8,128)} %inverses.1, f32[64,512]{1,0:T(8,128)} %coupling.1, bf16[2048,1024]{1,0:T(8,128)(2,1)} %design.1, f32[64,1024]{1,0:T(8,128)} %bitcast.6), custom_call_target="tpu_custom_call" | custom-call | tf_op jit(solution)/shard_map/pallas_call | solution.py:434
  42.2 1.4 %copy.11 = f32[128,64]{0,1:T(8,128)} copy(f32[128,64]{0,1:T(8,128)} %bitcast.8) | data formatting | bytes 65536
  43.6 1.3 %copy.12 = f32[1024]{0:T(1024)} copy(f32[1024]{0:T(1024)} %bitcast.9) | data formatting | bytes 8192
